TPU v7x, 32 devices: a whole 2x2x4 slice. The times are simulated.
32 devices in a mesh: gx: 8 (over z, x), gy: 4 (over y, core).
Axes of the slice: x: 2, y: 2, z: 4, core: 2. Of those that a mesh axis runs over, the one named last changes fastest.
Arguments:
- mode_fields: float32 [32, 512, 1024], P(None, 'gx', 'gy'), may hold values from -60 to 60, as said below
- conductance: float32 [512, 1024], P('gx', 'gy'), may hold values from 0.5 to 2
- potential: float32 [512, 1024], P('gx', 'gy'), may hold values from 0.25 to 4
Outputs:
- basis_field: float32 [128, 512, 1024], P(None, 'gx', 'gy')
- scaled_factor: float32 [128, 128], replicated
Inputs may be any that keep to these rules, and one draw needn't show every extreme that they name: `mode_fields`: Real-valued mode amplitudes.
All inputs are finite; a program needn't handle non-finite values.
Results may differ from a plain program's by a relative error of at most 0.0003.
Values sent between devices are 32-bit elements; how exact they have to be, the bound alone decides.
A program may use at most 64 MiB of HBM per device.

v0:
```python
import functools

import jax
import jax.numpy as jnp
from jax import lax
from jax.experimental import pallas as pl
from jax.experimental.pallas import tpu as pltpu
from jax.sharding import PartitionSpec as P

MESH = pl.DeviceIdType.MESH
F32 = jnp.float32
BF16 = jnp.bfloat16


def split(value):
    high = value.astype(BF16)
    return high, (value - high.astype(F32)).astype(BF16)


def gram_kernel(
    nx, ny, u_hbm, k_hbm, p_hbm, m_ref, g_ref,
    k_ref, p_ref, flat, load, wide, edge, halo, acc, part, piece, ring, full,
    halo_send, halo_recv, rs_send, rs_recv, all_send, all_recv, ag_send, ag_recv,
):
    rows, cols = k_hbm.shape
    modes = u_hbm.shape[0]
    tiles = cols // 128
    columns = 4 * modes
    share = columns // ny
    px, py = lax.axis_index("gx"), lax.axis_index("gy")

    loads = [
        pltpu.make_async_copy(
            u_hbm.at[:, pl.ds(q * 8, 8), pl.ds(t * 128, 128)], flat.at[t, q], load.at[t * (rows // 8) + q]
        )
        for q in range(rows // 8)
        for t in range(tiles)
    ]
    loads.append(pltpu.make_async_copy(k_hbm, k_ref, load.at[tiles * rows // 8]))
    loads.append(pltpu.make_async_copy(p_hbm, p_ref, load.at[tiles * rows // 8 + 1]))
    for copy in loads:
        copy.start()
    barrier = pltpu.get_barrier_semaphore()
    for d in range(1, nx):
        pl.semaphore_signal(barrier, inc=1, device_id={"gx": lax.rem(px + d, nx)}, device_id_type=MESH)
    for d in range(1, ny):
        pl.semaphore_signal(barrier, inc=1, device_id={"gy": lax.rem(py + d, ny)}, device_id_type=MESH)

    lanes = lax.broadcasted_iota(jnp.int32, (modes + 8, 128), 1)

    blocks = flat.reshape(tiles, rows // 8, modes * 8, 128)

    def spread(q, carry):
        first, last = carry
        for s in range(8):
            i = q * 8 + s
            row = jnp.concatenate(
                [jnp.concatenate([blocks[t, q, pl.ds(s, modes, stride=8), :] for t in range(tiles)], 1),
                 jnp.broadcast_to(k_ref[pl.ds(i, 1), :], (8, cols))], 0
            )
            wide[i + 1] = row
            first = jnp.where(lanes == i, pltpu.roll(row[:, :128], i, 1), first)
            last = jnp.where(lanes == i, pltpu.roll(row[:, cols - 128:], lax.rem(i + 1, 128), 1), last)
        return first, last

    for copy in loads:
        copy.wait()
    zero = jnp.zeros((modes + 8, 128), F32)
    first, last = lax.fori_loop(0, rows // 8, spread, (zero, zero))
    edge[0] = first
    edge[1] = last

    pl.semaphore_wait(barrier, nx + ny - 2)
    right, left = lax.rem(py + 1, ny), lax.rem(py + ny - 1, ny)
    down, up = lax.rem(px + 1, nx), lax.rem(px + nx - 1, nx)
    moves = (
        (edge.at[1], halo.at[0], {"gy": right}),
        (edge.at[0], halo.at[1], {"gy": left}),
        (wide.at[rows], wide.at[0], {"gx": down}),
        (wide.at[1], wide.at[rows + 1], {"gx": up}),
    )
    copies = [
        pltpu.make_async_remote_copy(
            src_ref=src, dst_ref=dst, send_sem=halo_send.at[n], recv_sem=halo_recv.at[n],
            device_id=device, device_id_type=MESH,
        )
        for n, (src, dst, device) in enumerate(moves)
    ]
    for copy in copies:
        copy.start()
    for copy in copies:
        copy.wait()
    wide[0] = jnp.where(px > 0, wide[0], 0.0)
    wide[rows + 1] = jnp.where(px < nx - 1, wide[rows + 1], 0.0)
    halo[0] = jnp.where(py > 0, halo[0], 0.0)
    halo[1] = jnp.where(py < ny - 1, halo[1], 0.0)

    group = 4
    span = lax.broadcasted_iota(jnp.int32, (modes + 8, cols), 1)
    acc[...] = jnp.zeros_like(acc)

    def build(g, _):
        for s in range(group):
            i = g * group + s
            row = wide[i + 1]
            center, k_mid = row[:modes], row[modes:modes + 1]
            after, before = wide[i + 2], wide[i]
            pad = jnp.zeros((modes + 8, cols - 128), F32)
            left_edge = jnp.concatenate([pltpu.roll(halo[0], lax.rem(128 - i, 128), 1), pad], 1)
            right_edge = jnp.concatenate([pad, pltpu.roll(halo[1], 127 - i, 1)], 1)
            to_left = jnp.where(span == 0, left_edge, pltpu.roll(row, 1, 1))
            to_right = jnp.where(span == cols - 1, right_edge, pltpu.roll(row, cols - 1, 1))
            along_x = (0.5 * (k_mid + after[modes:modes + 1])) * (center - after[:modes]) + (
                0.5 * (k_mid + before[modes:modes + 1])
            ) * (center - before[:modes])
            along_y = (0.5 * (k_mid + to_right[modes:modes + 1])) * (center - to_right[:modes]) + (
                0.5 * (k_mid + to_left[modes:modes + 1])
            ) * (center - to_left[:modes])
            react = p_ref[pl.ds(i, 1), :] * center
            high, low = split(jnp.concatenate([center, along_x, along_y, react], 0))
            for t in range(tiles):
                at = pl.ds(pl.multiple_of((t * rows + i) * 128, 128), 128)
                m_ref[:columns, at] = high[:, t * 128:(t + 1) * 128]
                m_ref[columns:, at] = low[:, t * 128:(t + 1) * 128]
        for t in range(tiles):
            at = pl.ds(pl.multiple_of((t * rows + g * group) * 128, group * 128), group * 128)
            acc[...] += lax.dot_general(
                m_ref[:columns, at], m_ref[:, at], (((1,), (1,)), ((), ())), preferred_element_type=F32
            )
        return 0

    lax.fori_loop(0, rows // group, build, 0)
    cross = acc[:, columns:]
    total = (acc[:, :columns] + (cross + cross.T)) * (1.0 / (rows * cols * nx * ny))
    for j in range(ny):
        part[j] = total[j * share:(j + 1) * share]

    copies = [
        pltpu.make_async_remote_copy(
            src_ref=part.at[lax.rem(py + d, ny)], dst_ref=piece.at[py], send_sem=rs_send.at[d], recv_sem=rs_recv.at[d],
            device_id={"gy": lax.rem(py + d, ny)}, device_id_type=MESH,
        )
        for d in range(1, ny)
    ]
    for copy in copies:
        copy.start()
    piece[py] = part[py]
    for copy in copies:
        copy.wait()
    ring[px] = functools.reduce(jnp.add, [piece[j] for j in range(ny)])

    copies = [
        pltpu.make_async_remote_copy(
            src_ref=ring.at[px], dst_ref=ring.at[px], send_sem=all_send.at[d], recv_sem=all_recv.at[d],
            device_id={"gx": lax.rem(px + d, nx)}, device_id_type=MESH,
        )
        for d in range(1, nx)
    ]
    for copy in copies:
        copy.start()
    for copy in copies:
        copy.wait()
    full[py] = functools.reduce(jnp.add, [ring[j] for j in range(nx)])

    copies = [
        pltpu.make_async_remote_copy(
            src_ref=full.at[py], dst_ref=full.at[py], send_sem=ag_send.at[d], recv_sem=ag_recv.at[d],
            device_id={"gy": lax.rem(py + d, ny)}, device_id_type=MESH,
        )
        for d in range(1, ny)
    ]
    for copy in copies:
        copy.start()
    for copy in copies:
        copy.wait()
    for j in range(ny):
        g_ref[j * share:(j + 1) * share, :] = full[j]


def gram(fields, conduct, potential, nx, ny):
    modes, rows, cols = fields.shape
    columns = 4 * modes
    vmem = pl.BlockSpec(memory_space=pltpu.VMEM)
    dma = pltpu.SemaphoreType.DMA
    return pl.pallas_call(
        functools.partial(gram_kernel, nx, ny),
        out_shape=(
            pltpu.VMEM((2 * columns, rows * cols), BF16),
            pltpu.VMEM((columns, columns), F32),
        ),
        in_specs=[pl.BlockSpec(memory_space=pltpu.HBM)] * 3,
        out_specs=(vmem, vmem),
        scratch_shapes=[
            pltpu.VMEM((rows, cols), F32),
            pltpu.VMEM((rows, cols), F32),
            pltpu.VMEM((cols // 128, rows // 8, modes, 8, 128), F32),
            dma((cols // 128 * rows // 8 + 2,)),
            pltpu.VMEM((rows + 2, modes + 8, cols), F32),
            pltpu.VMEM((2, modes + 8, 128), F32),
            pltpu.VMEM((2, modes + 8, 128), F32),
            pltpu.VMEM((columns, 2 * columns), F32),
            pltpu.VMEM((ny, columns // ny, columns), F32),
            pltpu.VMEM((ny, columns // ny, columns), F32),
            pltpu.VMEM((nx, columns // ny, columns), F32),
            pltpu.VMEM((ny, columns // ny, columns), F32),
            dma((4,)), dma((4,)), dma((ny,)), dma((ny,)), dma((nx,)), dma((nx,)), dma((ny,)), dma((ny,)),
        ],
        compiler_params=pltpu.CompilerParams(
            collective_id=0, has_side_effects=True, vmem_limit_bytes=28 * 1024 * 1024
        ),
        name="gram",
    )(*(pltpu.with_memory_space_constraint(a, pltpu.HBM) for a in (fields, conduct, potential)))


def factor(g_ref, r_ref, w_ref):
    size = g_ref.shape[0]
    block = 8
    panels = size // block
    lane = lax.broadcasted_iota(jnp.int32, (block, size), 1)
    sub = lax.broadcasted_iota(jnp.int32, (block, size), 0)

    def stack(values):
        out = values[0]
        for j in range(1, block):
            out = jnp.where(sub == j, values[j], out)
        return out

    def row(value, j):
        return jnp.broadcast_to(value[j:j + 1], (block, size))

    def column(value, j):
        return jnp.broadcast_to(value[:, j:j + 1], (block, size))

    z = [g_ref[i * block:(i + 1) * block, :] for i in range(panels)]
    for p in range(panels):
        at = p * block
        diag = [column(z[p], at + j) for j in range(block)]
        a = [[row(diag[j], i) for j in range(i + 1)] for i in range(block)]
        low = [[None] * block for _ in range(block)]
        inv = [[None] * block for _ in range(block)]
        for j in range(block):
            root = lax.rsqrt(a[j][j])
            inv[j][j] = root
            for i in range(j + 1, block):
                low[i][j] = a[i][j] * root
            for i in range(j + 1, block):
                for k in range(j + 1, i + 1):
                    a[i][k] = a[i][k] - low[i][j] * low[k][j]
            for k in range(j):
                terms = [low[j][q] * inv[q][k] for q in range(k, j)]
                inv[j][k] = -root * functools.reduce(jnp.add, terms)
        inside = (lane >= at) & (lane < at + block)
        source = [row(z[p], k) for k in range(block)]
        swept = [jnp.where(inside, jnp.where(lane == at + k, 1.0, 0.0), source[k]) for k in range(block)]
        solved = [functools.reduce(jnp.add, [inv[j][k] * swept[k] for k in range(j + 1)]) for j in range(block)]
        upper = [functools.reduce(jnp.add, [inv[j][k] * source[k] for k in range(j + 1)]) for j in range(block)]
        r_ref[at:at + block, :] = jnp.where(lane >= at + sub, stack(upper), 0.0)
        w_ref[at:at + block, :] = jnp.where(lane <= at + sub, stack(solved), 0.0)
        if p + 1 < panels:
            both = [
                functools.reduce(jnp.add, [inv[j][k] * solved[j] for j in range(k, block)]) for k in range(block)
            ]
            for i in range(p + 1, panels):
                terms = [column(z[i], at + k) * both[k] for k in range(block)]
                z[i] = jnp.where(inside, 0.0, z[i]) - functools.reduce(jnp.add, terms)


def apply_kernel(g_ref, m_ref, o_hbm, r_ref, w_ref, weights, out, sent):
    parts, columns, chunk, _ = out.shape
    per = o_hbm.shape[1] // chunk
    factor(g_ref, r_ref, w_ref)
    high, low = split(w_ref[...])
    weights[:columns, :columns] = high
    weights[:columns, columns:] = high
    weights[columns:, :columns] = low
    weights[columns:, columns:] = jnp.zeros_like(low)
    flat = out.reshape(parts, columns * chunk, 128)

    def send(q):
        to = o_hbm.at[:, pl.ds(lax.rem(q, per) * chunk, chunk), pl.ds(pl.multiple_of(q // per * 128, 128), 128)]
        return pltpu.make_async_copy(out.at[q], to, sent.at[q])

    def step(q, _):
        for s in range(0, chunk, 2):
            at = pl.ds(pl.multiple_of((q * chunk + s) * 128, 256), 256)
            both = jnp.dot(weights[...], m_ref[:, at], preferred_element_type=F32)
            value = both[:columns] + both[columns:]
            for r in range(2):
                flat[q, pl.ds(s + r, columns, stride=chunk), :] = value[:, r * 128:(r + 1) * 128]
        send(q).start()
        return 0

    def finish(q, _):
        send(q).wait()
        return 0

    lax.fori_loop(0, parts, step, 0)
    lax.fori_loop(0, parts, finish, 0)


def apply(total, matrix, rows, cols):
    columns = total.shape[0]
    chunk = 8
    parts = (rows // chunk) * (cols // 128)
    vmem = pl.BlockSpec(memory_space=pltpu.VMEM)
    return pl.pallas_call(
        apply_kernel,
        out_shape=(
            jax.ShapeDtypeStruct((columns, rows, cols), F32),
            jax.ShapeDtypeStruct((columns, columns), F32),
        ),
        in_specs=[vmem, vmem],
        out_specs=(pl.BlockSpec(memory_space=pltpu.HBM), vmem),
        scratch_shapes=[
            pltpu.VMEM((columns, columns), F32),
            pltpu.VMEM((2 * columns, 2 * columns), BF16),
            pltpu.VMEM((parts, columns, chunk, 128), F32),
            pltpu.SemaphoreType.DMA((parts,)),
        ],
        compiler_params=pltpu.CompilerParams(vmem_limit_bytes=20 * 1024 * 1024),
        name="apply",
    )(total, pltpu.with_memory_space_constraint(matrix, pltpu.VMEM))


def on_device(nx, ny, mode_fields, conductance, potential):
    _, rows, cols = mode_fields.shape
    matrix, total = gram(mode_fields, conductance, potential, nx, ny)
    return apply(total, matrix, rows, cols)


def solution(mesh):
    placed = (P(None, "gx", "gy"), P("gx", "gy"), P("gx", "gy"))
    return jax.shard_map(
        functools.partial(on_device, mesh.shape["gx"], mesh.shape["gy"]),
        mesh=mesh, in_specs=placed, out_specs=(P(None, "gx", "gy"), P()), check_vma=False,
    )
```

profile of v0, /device:TPU:0, one launch (start us, length us, event | category | flops | bytes accessed | tf_op | source)
XLA Modules:
  0.0 42.3 jit_solution(16510508666322547384)
XLA Ops:
  0.6 30.3 %gram.1 = (bf16[256,16384]{1,0:T(8,128)(2,1)S(1)}, f32[128,128]{1,0:T(8,128)S(1)}) custom-call(f32[32,64,256]{2,1,0:T(8,128)} %u_hbm.1, f32[64,256]{1,0:T(8,128)} %k_hbm.1, f32[64,256]{1,0:T(8,128)} %p_hbm.1), custom_call_target="tpu_custom_call" | custom-call | tf_op jit(solution)/shard_map/gram/pallas_call | solution.py:185
  31.0 11.3 %apply.1 = (f32[128,64,256]{2,1,0:T(8,128)}, f32[128,128]{1,0:T(8,128)}) custom-call(f32[128,128]{1,0:T(8,128)S(1)} %get-tuple-element.4.g_ref, bf16[256,16384]{1,0:T(8,128)(2,1)S(1)} %get-tuple-element.5.m_ref), custom_call_target="tpu_custom_call" | custom-call | tf_op jit(solution)/shard_map/apply/pallas_call | solution.py:306
where the time goes:
time: 42.4 us; the launch traced here: 42.3 us
  Pallas kernels  41.7 us (98%)
  between operations  0.64 us (2%)
    pallas_call x1, Pallas kernels, gram(): pl.pallas_call(functools.partial(gram_kernel, nx, ny), out_shape=(pltpu.V...  30.3 us
    pallas_call x1, Pallas kernels, apply(): pl.pallas_call(apply_kernel, out_shape=(jax.ShapeDtypeStruct((columns, ro...  11.3 us

commit v1 on v0

v1 whole, which is shorter than its diff:
```python
import functools

import jax
import jax.numpy as jnp
from jax import lax
from jax.experimental import pallas as pl
from jax.experimental.pallas import tpu as pltpu
from jax.sharding import PartitionSpec as P

MESH = pl.DeviceIdType.MESH
F32 = jnp.float32
BF16 = jnp.bfloat16


def split(value):
    high = value.astype(BF16)
    return high, (value - high.astype(F32)).astype(BF16)


def gram_kernel(
    nx, ny, u_hbm, k_hbm, p_hbm, m_ref, g_ref,
    wide, kappa, p_ref, xface, yface, yleft, edge, halo, kside, acc, part, piece, ring, full,
    load, halo_send, halo_recv, rs_send, rs_recv, all_send, all_recv, ag_send, ag_recv,
):
    rows, cols = k_hbm.shape
    modes = u_hbm.shape[0]
    tiles = cols // 128
    columns = 4 * modes
    share = columns // ny
    px, py = lax.axis_index("gx"), lax.axis_index("gy")

    def fetch(i):
        return pltpu.make_async_copy(u_hbm.at[:, i, :], wide.at[i + 1], load.at[i])

    coefs = [
        pltpu.make_async_copy(k_hbm, kappa.at[pl.ds(8, rows)], load.at[rows]),
        pltpu.make_async_copy(p_hbm, p_ref, load.at[rows + 1]),
    ]

    def begin(i, _):
        fetch(i).start()
        return 0

    lax.fori_loop(0, rows, begin, 0)
    for copy in coefs:
        copy.start()
    barrier = pltpu.get_barrier_semaphore()
    for d in range(1, nx):
        pl.semaphore_signal(barrier, inc=1, device_id={"gx": lax.rem(px + d, nx)}, device_id_type=MESH)
    for d in range(1, ny):
        pl.semaphore_signal(barrier, inc=1, device_id={"gy": lax.rem(py + d, ny)}, device_id_type=MESH)

    lanes = lax.broadcasted_iota(jnp.int32, (modes, 128), 1)

    def collect(q, carry):
        first, last = carry
        for s in range(8):
            fetch(q * 8 + s).wait()
        for s in range(8):
            i = q * 8 + s
            first = jnp.where(lanes == i, pltpu.roll(wide[i + 1, :, :128], i, 1), first)
            last = jnp.where(lanes == i, pltpu.roll(wide[i + 1, :, cols - 128:], (i + 1) & 127, 1), last)
        return first, last

    zero = jnp.zeros((modes, 128), F32)
    first, last = lax.fori_loop(0, rows // 8, collect, (zero, zero))
    edge[0] = first
    edge[1] = last
    for copy in coefs:
        copy.wait()

    pl.semaphore_wait(barrier, nx + ny - 2)
    has_up, has_down, has_left, has_right = px > 0, px < nx - 1, py > 0, py < ny - 1
    down, up = {"gx": lax.rem(px + 1, nx)}, {"gx": lax.rem(px + nx - 1, nx)}
    right, left = {"gy": lax.rem(py + 1, ny)}, {"gy": lax.rem(py + ny - 1, ny)}
    own = pl.ds(8, rows)
    moves = (
        (wide.at[rows], wide.at[0], down, has_down, has_up),
        (kappa.at[pl.ds(rows, 8)], kappa.at[pl.ds(0, 8)], down, has_down, has_up),
        (wide.at[1], wide.at[rows + 1], up, has_up, has_down),
        (kappa.at[pl.ds(8, 8)], kappa.at[pl.ds(rows + 8, 8)], up, has_up, has_down),
        (edge.at[1], halo.at[0], right, has_right, has_left),
        (kappa.at[own, pl.ds(cols - 128, 128)], kside.at[0], right, has_right, has_left),
        (edge.at[0], halo.at[1], left, has_left, has_right),
        (kappa.at[own, pl.ds(0, 128)], kside.at[1], left, has_left, has_right),
    )
    copies = [
        (
            pltpu.make_async_remote_copy(
                src_ref=src, dst_ref=dst, send_sem=halo_send.at[n], recv_sem=halo_recv.at[n],
                device_id=device, device_id_type=MESH,
            ), sends, receives,
        )
        for n, (src, dst, device, sends, receives) in enumerate(moves)
    ]
    for n in range(0, len(copies), 2):
        @pl.when(copies[n][1])
        def _():
            copies[n][0].start()
            copies[n + 1][0].start()

    def put(block, i, value):
        high, low = split(value)
        at = pl.ds(pl.multiple_of(i * cols, cols), cols)
        m_ref[block * modes:(block + 1) * modes, at] = high
        m_ref[columns + block * modes:columns + (block + 1) * modes, at] = low

    def flux(i):
        return xface[pl.ds(i, 1), :] * (wide[i] - wide[i + 1])

    def inner(i, before):
        after = flux(i + 1)
        center = wide[i + 1]
        put(0, i, center)
        put(1, i, after - before)
        put(3, i, p_ref[pl.ds(i, 1), :] * center)
        return after

    xface[pl.ds(1, rows - 1), :] = 0.5 * (kappa[pl.ds(8, rows - 1), :] + kappa[pl.ds(9, rows - 1), :])

    def pair(g, before):
        return inner(2 * g + 2, inner(2 * g + 1, before))

    lax.fori_loop(0, (rows - 2) // 2, pair, flux(1))

    for copy, sends, receives in copies:
        @pl.when(sends)
        def _():
            copy.wait_send()

        @pl.when(receives)
        def _():
            copy.wait_recv()

    @pl.when(px == 0)
    def _():
        wide[0] = jnp.zeros((modes, cols), F32)
        kappa[pl.ds(0, 8), :] = jnp.zeros((8, cols), F32)

    @pl.when(px == nx - 1)
    def _():
        wide[rows + 1] = jnp.zeros((modes, cols), F32)
        kappa[pl.ds(rows + 8, 8), :] = jnp.zeros((8, cols), F32)

    @pl.when(py == 0)
    def _():
        halo[0] = zero
        kside[0] = jnp.zeros((rows, 128), F32)

    @pl.when(py == ny - 1)
    def _():
        halo[1] = zero
        kside[1] = jnp.zeros((rows, 128), F32)

    for i in (0, rows):
        xface[i:i + 1, :] = 0.5 * (kappa[i + 7:i + 8, :] + kappa[i + 8:i + 9, :])
    inner(0, flux(0))
    inner(rows - 1, flux(rows - 1))

    lane = lax.broadcasted_iota(jnp.int32, (rows, 128), 1)
    k_tile = [kappa[own, t * 128:(t + 1) * 128] for t in range(tiles)]
    turned = [pltpu.roll(k, 127, 1) for k in k_tile] + [pltpu.roll(kside[1], 127, 1)]
    for t in range(tiles):
        yface[:, t * 128:(t + 1) * 128] = 0.5 * (k_tile[t] + jnp.where(lane == 127, turned[t + 1], turned[t]))
    yleft[...] = 0.5 * (pltpu.roll(kside[0], 1, 1) + k_tile[0])

    group = 4
    acc[...] = jnp.zeros_like(acc)

    def product(g):
        at = pl.ds(pl.multiple_of(g * group * cols, group * cols), group * cols)
        acc[...] += lax.dot_general(
            m_ref[:columns, at], m_ref[:, at], (((1,), (1,)), ((), ())), preferred_element_type=F32
        )

    def build(g):
        for s in range(group):
            i = g * group + s
            u = [wide[i + 1, :, t * 128:(t + 1) * 128] for t in range(tiles)]
            r = [pltpu.roll(value, 127, 1) for value in u] + [pltpu.roll(halo[1], 127 - i, 1)]
            scale = yface[pl.ds(i, 1), :]
            f = [
                scale[:, t * 128:(t + 1) * 128] * (u[t] - jnp.where(lanes == 127, r[t + 1], r[t]))
                for t in range(tiles)
            ]
            outer = yleft[pl.ds(i, 1), :] * (pltpu.roll(halo[0], (128 - i) & 127, 1) - u[0])
            b = [outer] + [pltpu.roll(value, 1, 1) for value in f]
            along = [f[t] - jnp.where(lanes == 0, b[t], b[t + 1]) for t in range(tiles)]
            put(2, i, jnp.concatenate(along, 1))

    def advance(g, _):
        product(g - 1)
        build(g)
        return 0

    build(0)
    lax.fori_loop(1, rows // group, advance, 0)
    product(rows // group - 1)
    cross = acc[:, columns:]
    total = (acc[:, :columns] + (cross + cross.T)) * (1.0 / (rows * cols * nx * ny))
    for j in range(ny):
        part[j] = total[j * share:(j + 1) * share]

    copies = [
        pltpu.make_async_remote_copy(
            src_ref=part.at[lax.rem(py + d, ny)], dst_ref=piece.at[py], send_sem=rs_send.at[d], recv_sem=rs_recv.at[d],
            device_id={"gy": lax.rem(py + d, ny)}, device_id_type=MESH,
        )
        for d in range(1, ny)
    ]
    for copy in copies:
        copy.start()
    piece[py] = part[py]
    for copy in copies:
        copy.wait()
    ring[px] = functools.reduce(jnp.add, [piece[j] for j in range(ny)])

    copies = [
        pltpu.make_async_remote_copy(
            src_ref=ring.at[px], dst_ref=ring.at[px], send_sem=all_send.at[d], recv_sem=all_recv.at[d],
            device_id={"gx": lax.rem(px + d, nx)}, device_id_type=MESH,
        )
        for d in range(1, nx)
    ]
    for copy in copies:
        copy.start()
    for copy in copies:
        copy.wait()
    full[py] = functools.reduce(jnp.add, [ring[j] for j in range(nx)])

    copies = [
        pltpu.make_async_remote_copy(
            src_ref=full.at[py], dst_ref=full.at[py], send_sem=ag_send.at[d], recv_sem=ag_recv.at[d],
            device_id={"gy": lax.rem(py + d, ny)}, device_id_type=MESH,
        )
        for d in range(1, ny)
    ]
    for copy in copies:
        copy.start()
    for copy in copies:
        copy.wait()
    for j in range(ny):
        g_ref[j * share:(j + 1) * share, :] = full[j]


def gram(fields, conduct, potential, nx, ny):
    modes, rows, cols = fields.shape
    columns = 4 * modes
    vmem = pl.BlockSpec(memory_space=pltpu.VMEM)
    dma = pltpu.SemaphoreType.DMA
    return pl.pallas_call(
        functools.partial(gram_kernel, nx, ny),
        out_shape=(
            pltpu.VMEM((2 * columns, rows * cols), BF16),
            pltpu.VMEM((columns, columns), F32),
        ),
        in_specs=[pl.BlockSpec(memory_space=pltpu.HBM)] * 3,
        out_specs=(vmem, vmem),
        scratch_shapes=[
            pltpu.VMEM((rows + 2, modes, cols), F32),
            pltpu.VMEM((rows + 16, cols), F32),
            pltpu.VMEM((rows, cols), F32),
            pltpu.VMEM((rows + 8, cols), F32),
            pltpu.VMEM((rows, cols), F32),
            pltpu.VMEM((rows, 128), F32),
            pltpu.VMEM((2, modes, 128), F32),
            pltpu.VMEM((2, modes, 128), F32),
            pltpu.VMEM((2, rows, 128), F32),
            pltpu.VMEM((columns, 2 * columns), F32),
            pltpu.VMEM((ny, columns // ny, columns), F32),
            pltpu.VMEM((ny, columns // ny, columns), F32),
            pltpu.VMEM((nx, columns // ny, columns), F32),
            pltpu.VMEM((ny, columns // ny, columns), F32),
            dma((rows + 2,)),
            dma((8,)), dma((8,)), dma((ny,)), dma((ny,)), dma((nx,)), dma((nx,)), dma((ny,)), dma((ny,)),
        ],
        compiler_params=pltpu.CompilerParams(
            collective_id=0, has_side_effects=True, vmem_limit_bytes=28 * 1024 * 1024
        ),
        name="gram",
    )(*(pltpu.with_memory_space_constraint(a, pltpu.HBM) for a in (fields, conduct, potential)))


def factor(g_ref, r_ref, w_ref):
    size = g_ref.shape[0]
    block = 8
    panels = size // block
    lane = lax.broadcasted_iota(jnp.int32, (block, size), 1)
    sub = lax.broadcasted_iota(jnp.int32, (block, size), 0)

    def row(value, j):
        return jnp.broadcast_to(value[j:j + 1], (block, size))

    def column(value, j):
        return jnp.broadcast_to(value[:, j:j + 1], (block, size))

    z = [g_ref[i * block:(i + 1) * block, :] for i in range(panels)]
    for p in range(panels):
        at = p * block
        inside = (lane >= at) & (lane < at + block)
        cols = [column(z[p], at + j) for j in range(block)]
        plain = z[p]
        swept = jnp.where(inside, jnp.where(lane == at + sub, 1.0, 0.0), plain)
        solved = upper = jnp.zeros((block, size), F32)
        for j in range(block):
            root = lax.rsqrt(row(cols[j], j))
            low = cols[j] * root
            both = jnp.where(sub == j, -root, low)
            for k in range(j + 1, block):
                cols[k] = jnp.where(sub == j, 0.0, cols[k]) - both * row(low, k)
            line = row(swept, j) * root
            solved = jnp.where(sub == j, line, solved)
            swept = jnp.where(sub == j, 0.0, swept) - both * line
            line = row(plain, j) * root
            upper = jnp.where(sub == j, line, upper)
            plain = plain - low * line
        r_ref[at:at + block, :] = jnp.where(lane >= at + sub, upper, 0.0)
        w_ref[at:at + block, :] = jnp.where(lane <= at + sub, solved, 0.0)
        lines = [row(swept, k) for k in range(block)]
        heads = [[column(z[i], at + k) for i in range(p + 1, panels)] for k in range(block)]
        for i in range(p + 1, panels):
            terms = [heads[k][i - p - 1] * lines[k] for k in range(block)]
            z[i] = jnp.where(inside, 0.0, z[i]) - functools.reduce(jnp.add, terms)


def apply_kernel(g_ref, m_ref, o_hbm, r_ref, w_ref, weights, out, sent):
    rows, columns, cols = out.shape
    factor(g_ref, r_ref, w_ref)
    high, low = split(w_ref[...])
    weights[:columns, :columns] = high
    weights[:columns, columns:] = high
    weights[columns:, :columns] = low
    weights[columns:, columns:] = jnp.zeros_like(low)
    group = 16

    def send(i):
        return pltpu.make_async_copy(out.at[i], o_hbm.at[:, i, :], sent.at[i])

    def step(g, _):
        for s in range(group):
            i = g * group + s
            at = pl.ds(pl.multiple_of(i * cols, cols), cols)
            both = jnp.dot(weights[...], m_ref[:, at], preferred_element_type=F32)
            out[i] = both[:columns] + both[columns:]
        for s in range(group):
            send(g * group + s).start()
        return 0

    def finish(i, _):
        send(i).wait()
        return 0

    lax.fori_loop(0, rows // group, step, 0)
    lax.fori_loop(0, rows, finish, 0)


def apply(total, matrix, rows, cols):
    columns = total.shape[0]
    vmem = pl.BlockSpec(memory_space=pltpu.VMEM)
    return pl.pallas_call(
        apply_kernel,
        out_shape=(
            jax.ShapeDtypeStruct((columns, rows, cols), F32),
            jax.ShapeDtypeStruct((columns, columns), F32),
        ),
        in_specs=[vmem, vmem],
        out_specs=(pl.BlockSpec(memory_space=pltpu.HBM), vmem),
        scratch_shapes=[
            pltpu.VMEM((columns, columns), F32),
            pltpu.VMEM((2 * columns, 2 * columns), BF16),
            pltpu.VMEM((rows, columns, cols), F32),
            pltpu.SemaphoreType.DMA((rows,)),
        ],
        compiler_params=pltpu.CompilerParams(vmem_limit_bytes=20 * 1024 * 1024),
        name="apply",
    )(total, pltpu.with_memory_space_constraint(matrix, pltpu.VMEM))


def on_device(nx, ny, mode_fields, conductance, potential):
    _, rows, cols = mode_fields.shape
    matrix, total = gram(mode_fields, conductance, potential, nx, ny)
    return apply(total, matrix, rows, cols)


def solution(mesh):
    placed = (P(None, "gx", "gy"), P("gx", "gy"), P("gx", "gy"))
    return jax.shard_map(
        functools.partial(on_device, mesh.shape["gx"], mesh.shape["gy"]),
        mesh=mesh, in_specs=placed, out_specs=(P(None, "gx", "gy"), P()), check_vma=False,
    )
```

time: 42.4 us -> 36.8 us (0.87)
  Pallas kernels: 41.7 us -> 36 us
    pallas_call x1, Pallas kernels: 30.3 us -> 26 us  [gram(): pl.pallas_call(functools.partial(gram_kernel, nx, ny), out_shape=(pltpu.V...]
    pallas_call x1, Pallas kernels: 11.3 us -> 10 us  [apply(): pl.pallas_call(apply_kernel, out_shape=(jax.ShapeDtypeStruct((columns, ro...]
where the time goes in v1:
time: 36.8 us; the launch traced here: 36.7 us
  Pallas kernels  36 us (98%)
  between operations  0.64 us (2%)
    pallas_call x1, Pallas kernels, gram(): pl.pallas_call(functools.partial(gram_kernel, nx, ny), out_shape=(pltpu.V...  26 us
    pallas_call x1, Pallas kernels, apply(): pl.pallas_call(apply_kernel, out_shape=(jax.ShapeDtypeStruct((columns, ro...  10 us

profile of v1, /device:TPU:0, one launch (start us, length us, event | category | flops | bytes accessed | tf_op | source)
XLA Modules:
  0.0 36.7 jit_solution(12556043101064192804)
XLA Ops:
  0.6 26.0 %gram.1 = (bf16[256,16384]{1,0:T(8,128)(2,1)S(1)}, f32[128,128]{1,0:T(8,128)S(1)}) custom-call(f32[32,64,256]{2,1,0:T(8,128)} %u_hbm.1, f32[64,256]{1,0:T(8,128)} %k_hbm.1, f32[64,256]{1,0:T(8,128)} %p_hbm.1), custom_call_target="tpu_custom_call" | custom-call | tf_op jit(solution)/shard_map/gram/pallas_call | solution.py:251
  26.7 10.0 %apply.1 = (f32[128,64,256]{2,1,0:T(8,128)}, f32[128,128]{1,0:T(8,128)}) custom-call(f32[128,128]{1,0:T(8,128)S(1)} %get-tuple-element.4.g_ref, bf16[256,16384]{1,0:T(8,128)(2,1)S(1)} %get-tuple-element.5.m_ref), custom_call_target="tpu_custom_call" | custom-call | tf_op jit(solution)/shard_map/apply/pallas_call | solution.py:360

commit v2 on v1

v2 whole, which is shorter than its diff:
```python
import functools

import jax
import jax.numpy as jnp
from jax import lax
from jax.experimental import pallas as pl
from jax.experimental.pallas import tpu as pltpu
from jax.sharding import PartitionSpec as P

MESH = pl.DeviceIdType.MESH
F32 = jnp.float32
BF16 = jnp.bfloat16


def split(value):
    high = value.astype(BF16)
    return high, (value - high.astype(F32)).astype(BF16)


def gram_kernel(
    nx, ny, u_hbm, k_hbm, p_hbm, m_ref, g_ref,
    wide, kappa, p_ref, xface, yface, edge, halo, inside, acc, part, piece, ring, full,
    load, halo_send, halo_recv, rs_send, rs_recv, all_send, all_recv, ag_send, ag_recv,
):
    rows, cols = k_hbm.shape
    modes = u_hbm.shape[0]
    tiles = cols // 128
    columns = 4 * modes
    share = columns // ny
    px, py = lax.axis_index("gx"), lax.axis_index("gy")

    def fetch(i):
        return pltpu.make_async_copy(u_hbm.at[:, i, :], wide.at[i + 1], load.at[i])

    own = pl.ds(8, rows)
    load_k = pltpu.make_async_copy(k_hbm, kappa.at[own], load.at[rows])
    load_p = pltpu.make_async_copy(p_hbm, p_ref, load.at[rows + 1])

    def begin(i, _):
        fetch(i).start()
        return 0

    load_k.start()
    lax.fori_loop(0, rows, begin, 0)
    load_p.start()
    barrier = pltpu.get_barrier_semaphore()
    for d in range(1, nx):
        pl.semaphore_signal(barrier, inc=1, device_id={"gx": lax.rem(px + d, nx)}, device_id_type=MESH)
    for d in range(1, ny):
        pl.semaphore_signal(barrier, inc=1, device_id={"gy": lax.rem(py + d, ny)}, device_id_type=MESH)

    def iota(height):
        return lax.broadcasted_iota(jnp.int32, (height, 128), 1)

    lanes = iota(modes)
    packed = iota(modes + 8)
    holder = ((packed + 1) & 127) >> 1
    load_k.wait()

    def collect(q, pack):
        for s in range(8):
            fetch(q * 8 + s).wait()
        for s in range(8):
            i = q * 8 + s
            k_row = jnp.broadcast_to(kappa[pl.ds(i + 8, 1), :], (8, cols))
            first = jnp.concatenate([wide[i + 1, :, :128], k_row[:, :128]], 0)
            last = jnp.concatenate([wide[i + 1, :, cols - 128:], k_row[:, cols - 128:]], 0)
            pack = jnp.where(holder == i, pltpu.roll(jnp.where(packed == 0, first, last), 2 * i, 1), pack)
        return pack

    edge[...] = lax.fori_loop(0, rows // 8, collect, jnp.zeros((modes + 8, 128), F32))

    pl.semaphore_wait(barrier, nx + ny - 2)
    has_up, has_down, has_left, has_right = px > 0, px < nx - 1, py > 0, py < ny - 1
    down, up = {"gx": lax.rem(px + 1, nx)}, {"gx": lax.rem(px + nx - 1, nx)}
    right, left = {"gy": lax.rem(py + 1, ny)}, {"gy": lax.rem(py + ny - 1, ny)}
    moves = (
        (wide.at[rows], wide.at[0], down, has_down, has_up),
        (kappa.at[pl.ds(rows, 8)], kappa.at[pl.ds(0, 8)], down, has_down, has_up),
        (wide.at[1], wide.at[rows + 1], up, has_up, has_down),
        (kappa.at[pl.ds(8, 8)], kappa.at[pl.ds(rows + 8, 8)], up, has_up, has_down),
        (edge, halo.at[0], right, has_right, has_left),
        (edge, halo.at[1], left, has_left, has_right),
    )
    copies = [
        (
            pltpu.make_async_remote_copy(
                src_ref=src, dst_ref=dst, send_sem=halo_send.at[n], recv_sem=halo_recv.at[n],
                device_id=device, device_id_type=MESH,
            ), sends, receives,
        )
        for n, (src, dst, device, sends, receives) in enumerate(moves)
    ]
    for copy, sends, _ in copies:
        @pl.when(sends)
        def _():
            copy.start()

    def put(block, i, value):
        high, low = split(value)
        at = pl.ds(pl.multiple_of(i * cols, cols), cols)
        m_ref[block * modes:(block + 1) * modes, at] = high
        m_ref[columns + block * modes:columns + (block + 1) * modes, at] = low

    def flux(i):
        return xface[pl.ds(i, 1), :] * (wide[i] - wide[i + 1])

    xface[pl.ds(1, rows - 1), :] = 0.5 * (kappa[pl.ds(8, rows - 1), :] + kappa[pl.ds(9, rows - 1), :])
    lane = iota(rows)
    k_tile = [kappa[own, t * 128:(t + 1) * 128] for t in range(tiles)]
    turned = [pltpu.roll(k, 127, 1) for k in k_tile]
    for t in range(tiles):
        face = 0.5 * (k_tile[t] + (jnp.where(lane == 127, turned[t + 1], turned[t]) if t + 1 < tiles else turned[t]))
        yface[:, t * 128:(t + 1) * 128] = face if t + 1 < tiles else jnp.where(lane == 127, 0.0, face)
    load_p.wait()

    def local(i):
        center = wide[i + 1]
        put(0, i, center)
        put(3, i, p_ref[pl.ds(i, 1), :] * center)
        u = [center[:, t * 128:(t + 1) * 128] for t in range(tiles)]
        r = [pltpu.roll(value, 127, 1) for value in u]
        scale = yface[pl.ds(i, 1), :]
        f = [
            scale[:, t * 128:(t + 1) * 128] * (u[t] - (jnp.where(lanes == 127, r[t + 1], r[t]) if t + 1 < tiles else r[t]))
            for t in range(tiles)
        ]
        b = [pltpu.roll(value, 1, 1) for value in f]
        for t in range(tiles):
            inside[i, :, t * 128:(t + 1) * 128] = f[t] - jnp.where(lanes == 0, b[t - 1], b[t])

    group = 16

    def inner(first, count, before):
        for s in range(group):
            local(first + s)
            if s < count:
                after = flux(first + s + 2)
                put(1, first + s + 1, after - before)
                before = after
        return before

    def sweep(g, before):
        return inner(g * group, group, before)

    inner(rows - group, group - 2, lax.fori_loop(0, rows // group - 1, sweep, flux(1)))

    for copy, sends, receives in copies:
        @pl.when(sends)
        def _():
            copy.wait_send()

        @pl.when(receives)
        def _():
            copy.wait_recv()

    @pl.when(px == 0)
    def _():
        wide[0] = jnp.zeros((modes, cols), F32)
        kappa[pl.ds(0, 8), :] = jnp.zeros((8, cols), F32)

    @pl.when(px == nx - 1)
    def _():
        wide[rows + 1] = jnp.zeros((modes, cols), F32)
        kappa[pl.ds(rows + 8, 8), :] = jnp.zeros((8, cols), F32)

    @pl.when(py == 0)
    def _():
        halo[0] = jnp.zeros((modes + 8, 128), F32)

    @pl.when(py == ny - 1)
    def _():
        halo[1] = jnp.zeros((modes + 8, 128), F32)

    for i in (0, rows):
        xface[i:i + 1, :] = 0.5 * (kappa[i + 7:i + 8, :] + kappa[i + 8:i + 9, :])
    for i in (0, rows - 1):
        put(1, i, flux(i + 1) - flux(i))
    mine = edge[...]
    other = jnp.where((packed & 1) == 0, pltpu.roll(halo[0], 1, 1), pltpu.roll(halo[1], 127, 1))
    across = 0.5 * (mine[modes:modes + 1] + other[modes:modes + 1]) * (mine[:modes] - other[:modes])

    acc[...] = jnp.zeros_like(acc)

    def build(g, _):
        for s in range(group):
            i = g * group + s
            turn = pltpu.roll(across, (128 - 2 * i) & 127, 1)
            y = [inside[i, :, t * 128:(t + 1) * 128] for t in range(tiles)]
            y[0] = y[0] + jnp.where(lanes == 0, turn, 0.0)
            y[-1] = y[-1] + jnp.where(lanes == 127, turn, 0.0)
            put(2, i, jnp.concatenate(y, 1))
        at = pl.ds(pl.multiple_of(g * group * cols, group * cols), group * cols)
        acc[...] += lax.dot_general(
            m_ref[:, at], m_ref[:columns, at], (((1,), (1,)), ((), ())), preferred_element_type=F32
        )
        return 0

    lax.fori_loop(0, rows // group, build, 0)
    cross = acc[columns:]
    total = (acc[:columns] + (cross + cross.T)) * (1.0 / (rows * cols * nx * ny))
    for j in range(ny):
        part[j] = total[j * share:(j + 1) * share]

    copies = [
        pltpu.make_async_remote_copy(
            src_ref=part.at[lax.rem(py + d, ny)], dst_ref=piece.at[py], send_sem=rs_send.at[d], recv_sem=rs_recv.at[d],
            device_id={"gy": lax.rem(py + d, ny)}, device_id_type=MESH,
        )
        for d in range(1, ny)
    ]
    for copy in copies:
        copy.start()
    piece[py] = part[py]
    for copy in copies:
        copy.wait()
    ring[px] = functools.reduce(jnp.add, [piece[j] for j in range(ny)])

    copies = [
        pltpu.make_async_remote_copy(
            src_ref=ring.at[px], dst_ref=ring.at[px], send_sem=all_send.at[d], recv_sem=all_recv.at[d],
            device_id={"gx": lax.rem(px + d, nx)}, device_id_type=MESH,
        )
        for d in range(1, nx)
    ]
    for copy in copies:
        copy.start()
    for copy in copies:
        copy.wait()
    full[py] = functools.reduce(jnp.add, [ring[j] for j in range(nx)])

    copies = [
        pltpu.make_async_remote_copy(
            src_ref=full.at[py], dst_ref=full.at[py], send_sem=ag_send.at[d], recv_sem=ag_recv.at[d],
            device_id={"gy": lax.rem(py + d, ny)}, device_id_type=MESH,
        )
        for d in range(1, ny)
    ]
    for copy in copies:
        copy.start()
    for copy in copies:
        copy.wait()
    for j in range(ny):
        g_ref[j * share:(j + 1) * share, :] = full[j]


def gram(fields, conduct, potential, nx, ny):
    modes, rows, cols = fields.shape
    columns = 4 * modes
    vmem = pl.BlockSpec(memory_space=pltpu.VMEM)
    dma = pltpu.SemaphoreType.DMA
    return pl.pallas_call(
        functools.partial(gram_kernel, nx, ny),
        out_shape=(
            pltpu.VMEM((2 * columns, rows * cols), BF16),
            pltpu.VMEM((columns, columns), F32),
        ),
        in_specs=[pl.BlockSpec(memory_space=pltpu.HBM)] * 3,
        out_specs=(vmem, vmem),
        scratch_shapes=[
            pltpu.VMEM((rows + 2, modes, cols), F32),
            pltpu.VMEM((rows + 16, cols), F32),
            pltpu.VMEM((rows, cols), F32),
            pltpu.VMEM((rows + 8, cols), F32),
            pltpu.VMEM((rows, cols), F32),
            pltpu.VMEM((modes + 8, 128), F32),
            pltpu.VMEM((2, modes + 8, 128), F32),
            pltpu.VMEM((rows, modes, cols), F32),
            pltpu.VMEM((2 * columns, columns), F32),
            pltpu.VMEM((ny, columns // ny, columns), F32),
            pltpu.VMEM((ny, columns // ny, columns), F32),
            pltpu.VMEM((nx, columns // ny, columns), F32),
            pltpu.VMEM((ny, columns // ny, columns), F32),
            dma((rows + 2,)),
            dma((6,)), dma((6,)), dma((ny,)), dma((ny,)), dma((nx,)), dma((nx,)), dma((ny,)), dma((ny,)),
        ],
        compiler_params=pltpu.CompilerParams(
            collective_id=0, has_side_effects=True, vmem_limit_bytes=28 * 1024 * 1024
        ),
        name="gram",
    )(*(pltpu.with_memory_space_constraint(a, pltpu.HBM) for a in (fields, conduct, potential)))


def factor(g_ref, r_ref, w_ref):
    size = g_ref.shape[0]
    block, width = 8, 16
    parts, tiles = width // block, size // block
    lane = lax.broadcasted_iota(jnp.int32, (block, size), 1)
    sub = lax.broadcasted_iota(jnp.int32, (block, size), 0)

    def row(value, j):
        return jnp.broadcast_to(value[j:j + 1], (block, size))

    def column(value, j):
        return jnp.broadcast_to(value[:, j:j + 1], (block, size))

    z = [g_ref[i * block:(i + 1) * block, :] for i in range(tiles)]
    for at in range(0, size, width):
        if at == size // 2:
            yield
        start = at // block
        stop = start + parts
        inside = (lane >= at) & (lane < at + width)
        cols = [[column(value, at + k) for value in z[start:stop]] for k in range(width)]
        plain = z[start:stop]
        swept = [
            jnp.where(inside, jnp.where(lane == at + h * block + sub, 1.0, 0.0), value)
            for h, value in enumerate(plain)
        ]
        solved = [jnp.zeros((block, size), F32)] * parts
        upper = list(solved)
        for j in range(width):
            h, s = divmod(j, block)
            root = lax.rsqrt(row(cols[j][h], s))
            low = [value * root for value in cols[j]]
            both = list(low)
            both[h] = jnp.where(sub == s, -root, low[h])

            def sweep(values, line):
                return [
                    (jnp.where(sub == s, 0.0, value) if q == h else value) - both[q] * line
                    for q, value in enumerate(values)
                ]

            for k in range(j + 1, width):
                cols[k] = sweep(cols[k], row(low[k // block], k % block))
            line = row(swept[h], s) * root
            solved[h] = jnp.where(sub == s, line, solved[h])
            swept = sweep(swept, line)
            line = row(plain[h], s) * root
            upper[h] = jnp.where(sub == s, line, upper[h])
            plain = [value if q < h else value - low[q] * line for q, value in enumerate(plain)]
        for h in range(parts):
            first = at + h * block
            r_ref[first:first + block, :] = jnp.where(lane >= first + sub, upper[h], 0.0)
            w_ref[first:first + block, :] = jnp.where(lane <= first + sub, solved[h], 0.0)
        for i in range(stop, min(stop + parts, tiles)):
            terms = [column(z[i], at + k) * row(swept[k // block], k % block) for k in range(width)]
            while len(terms) > 1:
                terms = [x + y for x, y in zip(terms[::2], terms[1::2])]
            z[i] = jnp.where(inside, 0.0, z[i]) - terms[0]
        if stop + parts < tiles:
            pads = [jnp.zeros((at, size), F32)] * (at > 0)
            sides = jnp.concatenate(pads + swept + [jnp.zeros((size - at - width, size), F32)], 0)
            change = jnp.dot(
                jnp.concatenate(z[stop + parts:], 0), sides,
                preferred_element_type=F32, precision=lax.Precision.HIGHEST,
            )
            for n, i in enumerate(range(stop + parts, tiles)):
                z[i] = jnp.where(inside, 0.0, z[i]) - change[n * block:(n + 1) * block]
    yield


def apply_kernel(g_ref, m_ref, o_hbm, r_ref, w_ref, upper, lower, out, sent):
    rows, columns, cols = out.shape
    half = columns // 2
    group = 16
    steps = factor(g_ref, r_ref, w_ref)

    def send(side, i):
        part = pl.ds(side * half, half)
        return pltpu.make_async_copy(out.at[i, part], o_hbm.at[part, i, :], sent)

    def over(side, value):
        def step(g, _):
            for s in range(group):
                i = g * group + s
                out[i, side * half:(side + 1) * half, :] = value(pl.ds(pl.multiple_of(i * cols, cols), cols))
            for s in range(group):
                send(side, g * group + s).start()
            return 0

        lax.fori_loop(0, rows // group, step, 0)

    next(steps)
    high, low = split(w_ref[:half, :])
    upper[...] = jnp.concatenate([high[:, :half], high[:, :half], low[:, :half]], 1)

    def first(at):
        near = m_ref[:half, at]
        right = jnp.concatenate([near, m_ref[columns:columns + half, at], near], 0)
        return jnp.dot(upper[...], right, preferred_element_type=F32)

    over(0, first)
    next(steps)
    high, low = split(w_ref[half:, :])
    lower[:half, :columns] = high
    lower[:half, columns:] = high
    lower[half:, :columns] = low
    lower[half:, columns:] = jnp.zeros_like(low)

    def second(at):
        both = jnp.dot(lower[...], m_ref[:, at], preferred_element_type=F32)
        return both[:half] + both[half:]

    over(1, second)

    pltpu.make_async_copy(out, out, sent).wait()


def apply(total, matrix, rows, cols):
    columns = total.shape[0]
    vmem = pl.BlockSpec(memory_space=pltpu.VMEM)
    return pl.pallas_call(
        apply_kernel,
        out_shape=(
            jax.ShapeDtypeStruct((columns, rows, cols), F32),
            jax.ShapeDtypeStruct((columns, columns), F32),
        ),
        in_specs=[vmem, vmem],
        out_specs=(pl.BlockSpec(memory_space=pltpu.HBM), vmem),
        scratch_shapes=[
            pltpu.VMEM((columns, columns), F32),
            pltpu.VMEM((columns // 2, 3 * columns // 2), BF16),
            pltpu.VMEM((columns, 2 * columns), BF16),
            pltpu.VMEM((rows, columns, cols), F32),
            pltpu.SemaphoreType.DMA,
        ],
        compiler_params=pltpu.CompilerParams(vmem_limit_bytes=20 * 1024 * 1024),
        name="apply",
    )(total, pltpu.with_memory_space_constraint(matrix, pltpu.VMEM))


def on_device(nx, ny, mode_fields, conductance, potential):
    _, rows, cols = mode_fields.shape
    matrix, total = gram(mode_fields, conductance, potential, nx, ny)
    return apply(total, matrix, rows, cols)


def solution(mesh):
    placed = (P(None, "gx", "gy"), P("gx", "gy"), P("gx", "gy"))
    return jax.shard_map(
        functools.partial(on_device, mesh.shape["gx"], mesh.shape["gy"]),
        mesh=mesh, in_specs=placed, out_specs=(P(None, "gx", "gy"), P()), check_vma=False,
    )
```

time: 36.8 us -> 33.9 us (0.921)
  Pallas kernels: 36 us -> 33.1 us
    pallas_call x1, Pallas kernels: 10 us -> 8.34 us  [apply(): pl.pallas_call(apply_kernel, out_shape=(jax.ShapeDtypeStruct((columns, ro...]
    pallas_call x1, Pallas kernels: 26 us -> 24.8 us  [gram(): pl.pallas_call(functools.partial(gram_kernel, nx, ny), out_shape=(pltpu.V...]
where the time goes in v2:
time: 33.9 us; the launch traced here: 33.7 us
  Pallas kernels  33.1 us (98%)
  between operations  0.64 us (2%)
    pallas_call x1, Pallas kernels, gram(): pl.pallas_call(functools.partial(gram_kernel, nx, ny), out_shape=(pltpu.V...  24.8 us
    pallas_call x1, Pallas kernels, apply(): pl.pallas_call(apply_kernel, out_shape=(jax.ShapeDtypeStruct((columns, ro...  8.34 us

profile of v2, /device:TPU:0, one launch (start us, length us, event | category | flops | bytes accessed | tf_op | source)
XLA Modules:
  0.0 33.7 jit_solution(966971327076706105)
XLA Ops:
  0.6 24.8 %gram.1 = (bf16[256,16384]{1,0:T(8,128)(2,1)S(1)}, f32[128,128]{1,0:T(8,128)S(1)}) custom-call(f32[32,64,256]{2,1,0:T(8,128)} %u_hbm.1, f32[64,256]{1,0:T(8,128)} %k_hbm.1, f32[64,256]{1,0:T(8,128)} %p_hbm.1), custom_call_target="tpu_custom_call" | custom-call | tf_op jit(solution)/shard_map/gram/pallas_call | solution.py:252
  25.4 8.3 %apply.1 = (f32[128,64,256]{2,1,0:T(8,128)}, f32[128,128]{1,0:T(8,128)}) custom-call(f32[128,128]{1,0:T(8,128)S(1)} %get-tuple-element.4.g_ref, bf16[256,16384]{1,0:T(8,128)(2,1)S(1)} %get-tuple-element.5.m_ref), custom_call_target="tpu_custom_call" | custom-call | tf_op jit(solution)/shard_map/apply/pallas_call | solution.py:404

commit v3 on v2

--- a/solution.py
+++ b/solution.py
@@ -19,7 +19,7 @@
 
 def gram_kernel(
     nx, ny, u_hbm, k_hbm, p_hbm, m_ref, g_ref,
-    wide, kappa, p_ref, xface, yface, edge, halo, inside, acc, part, piece, ring, full,
+    wide, kappa, p_ref, xface, yface, edge, halo, turned, flow, back, acc, part, piece, ring, full,
     load, halo_send, halo_recv, rs_send, rs_recv, all_send, all_recv, ag_send, ag_recv,
 ):
     rows, cols = k_hbm.shape
@@ -107,10 +107,14 @@
 
     xface[pl.ds(1, rows - 1), :] = 0.5 * (kappa[pl.ds(8, rows - 1), :] + kappa[pl.ds(9, rows - 1), :])
     lane = iota(rows)
+
+    def tile(t):
+        return slice(t * 128, (t + 1) * 128)
+
     k_tile = [kappa[own, t * 128:(t + 1) * 128] for t in range(tiles)]
-    turned = [pltpu.roll(k, 127, 1) for k in k_tile]
+    k_next = [pltpu.roll(k, 127, 1) for k in k_tile]
     for t in range(tiles):
-        face = 0.5 * (k_tile[t] + (jnp.where(lane == 127, turned[t + 1], turned[t]) if t + 1 < tiles else turned[t]))
+        face = 0.5 * (k_tile[t] + (jnp.where(lane == 127, k_next[t + 1], k_next[t]) if t + 1 < tiles else k_next[t]))
         yface[:, t * 128:(t + 1) * 128] = face if t + 1 < tiles else jnp.where(lane == 127, 0.0, face)
     load_p.wait()
 
@@ -118,16 +122,20 @@
         center = wide[i + 1]
         put(0, i, center)
         put(3, i, p_ref[pl.ds(i, 1), :] * center)
-        u = [center[:, t * 128:(t + 1) * 128] for t in range(tiles)]
-        r = [pltpu.roll(value, 127, 1) for value in u]
-        scale = yface[pl.ds(i, 1), :]
-        f = [
-            scale[:, t * 128:(t + 1) * 128] * (u[t] - (jnp.where(lanes == 127, r[t + 1], r[t]) if t + 1 < tiles else r[t]))
-            for t in range(tiles)
-        ]
-        b = [pltpu.roll(value, 1, 1) for value in f]
         for t in range(tiles):
-            inside[i, :, t * 128:(t + 1) * 128] = f[t] - jnp.where(lanes == 0, b[t - 1], b[t])
+            turned[i, :, tile(t)] = pltpu.roll(center[:, tile(t)], 127, 1)
+
+    def stream(g, _):
+        for s in range(group):
+            i = g * group + s
+            scale = yface[pl.ds(i, 1), :]
+            r = [turned[i, :, tile(t)] for t in range(tiles)]
+            for t in range(tiles):
+                after = jnp.where(lanes == 127, r[t + 1], r[t]) if t + 1 < tiles else r[t]
+                f = scale[:, tile(t)] * (wide[i + 1, :, tile(t)] - after)
+                flow[i, :, tile(t)] = f
+                back[i, :, tile(t)] = pltpu.roll(f, 1, 1)
+        return 0
 
     group = 16
 
@@ -144,6 +152,7 @@
         return inner(g * group, group, before)
 
     inner(rows - group, group - 2, lax.fori_loop(0, rows // group - 1, sweep, flux(1)))
+    lax.fori_loop(0, rows // group, stream, 0)
 
     for copy, sends, receives in copies:
         @pl.when(sends)
@@ -183,20 +192,21 @@
     acc[...] = jnp.zeros_like(acc)
 
     def build(g, _):
-        for s in range(group):
-            i = g * group + s
+        for s in range(32):
+            i = g * 32 + s
             turn = pltpu.roll(across, (128 - 2 * i) & 127, 1)
-            y = [inside[i, :, t * 128:(t + 1) * 128] for t in range(tiles)]
+            b = [back[i, :, tile(t)] for t in range(tiles)]
+            y = [flow[i, :, tile(t)] - jnp.where(lanes == 0, b[t - 1], b[t]) for t in range(tiles)]
             y[0] = y[0] + jnp.where(lanes == 0, turn, 0.0)
             y[-1] = y[-1] + jnp.where(lanes == 127, turn, 0.0)
             put(2, i, jnp.concatenate(y, 1))
-        at = pl.ds(pl.multiple_of(g * group * cols, group * cols), group * cols)
+        at = pl.ds(pl.multiple_of(g * 32 * cols, 32 * cols), 32 * cols)
         acc[...] += lax.dot_general(
             m_ref[:, at], m_ref[:columns, at], (((1,), (1,)), ((), ())), preferred_element_type=F32
         )
         return 0
 
-    lax.fori_loop(0, rows // group, build, 0)
+    lax.fori_loop(0, rows // 32, build, 0)
     cross = acc[columns:]
     total = (acc[:columns] + (cross + cross.T)) * (1.0 / (rows * cols * nx * ny))
     for j in range(ny):
@@ -265,6 +275,8 @@
             pltpu.VMEM((rows, cols), F32),
             pltpu.VMEM((modes + 8, 128), F32),
             pltpu.VMEM((2, modes + 8, 128), F32),
+            pltpu.VMEM((rows, modes, cols), F32),
+            pltpu.VMEM((rows, modes, cols), F32),
             pltpu.VMEM((rows, modes, cols), F32),
             pltpu.VMEM((2 * columns, columns), F32),
             pltpu.VMEM((ny, columns // ny, columns), F32),
@@ -361,16 +373,16 @@
         part = pl.ds(side * half, half)
         return pltpu.make_async_copy(out.at[i, part], o_hbm.at[part, i, :], sent)
 
-    def over(side, value):
-        def step(g, _):
-            for s in range(group):
-                i = g * group + s
-                out[i, side * half:(side + 1) * half, :] = value(pl.ds(pl.multiple_of(i * cols, cols), cols))
-            for s in range(group):
-                send(side, g * group + s).start()
-            return 0
-
-        lax.fori_loop(0, rows // group, step, 0)
+    def over(side, value, groups, between=None):
+        first = 0
+        for size in groups:
+            for i in range(first, first + size):
+                out[i, side * half:(side + 1) * half, :] = value(slice(i * cols, (i + 1) * cols))
+                if between:
+                    between(i)
+            for i in range(first, first + size):
+                send(side, i).start()
+            first += size
 
     next(steps)
     high, low = split(w_ref[:half, :])
@@ -381,7 +393,7 @@
         right = jnp.concatenate([near, m_ref[columns:columns + half, at], near], 0)
         return jnp.dot(upper[...], right, preferred_element_type=F32)
 
-    over(0, first)
+    over(0, first, (rows,))
     next(steps)
     high, low = split(w_ref[half:, :])
     lower[:half, :columns] = high
@@ -393,7 +405,7 @@
         both = jnp.dot(lower[...], m_ref[:, at], preferred_element_type=F32)
         return both[:half] + both[half:]
 
-    over(1, second)
+    over(1, second, (rows // 2, rows // 4, rows // 4))
 
     pltpu.make_async_copy(out, out, sent).wait()
 

time: 33.9 us -> 31.4 us (0.926)
  Pallas kernels: 33.1 us -> 30.6 us
    pallas_call x1, Pallas kernels: 8.34 us -> 6.92 us  [apply(): pl.pallas_call(apply_kernel, out_shape=(jax.ShapeDtypeStruct((columns, ro...]
    pallas_call x1, Pallas kernels: 24.8 us -> 23.7 us  [gram(): pl.pallas_call(functools.partial(gram_kernel, nx, ny), out_shape=(pltpu.V...]
where the time goes in v3:
time: 31.4 us; the launch traced here: 31.2 us
  Pallas kernels  30.6 us (97%)
  between operations  0.64 us (2%)
    pallas_call x1, Pallas kernels, gram(): pl.pallas_call(functools.partial(gram_kernel, nx, ny), out_shape=(pltpu.V...  23.7 us
    pallas_call x1, Pallas kernels, apply(): pl.pallas_call(apply_kernel, out_shape=(jax.ShapeDtypeStruct((columns, ro...  6.92 us

profile of v3, /device:TPU:0, one launch (start us, length us, event | category | flops | bytes accessed | tf_op | source)
XLA Modules:
  0.0 31.2 jit_solution(8316829647987535930)
XLA Ops:
  0.6 23.7 %gram.1 = (bf16[256,16384]{1,0:T(8,128)(2,1)S(1)}, f32[128,128]{1,0:T(8,128)S(1)}) custom-call(f32[32,64,256]{2,1,0:T(8,128)} %u_hbm.1, f32[64,256]{1,0:T(8,128)} %k_hbm.1, f32[64,256]{1,0:T(8,128)} %p_hbm.1), custom_call_target="tpu_custom_call" | custom-call | tf_op jit(solution)/shard_map/gram/pallas_call | solution.py:262
  24.3 6.9 %apply.1 = (f32[128,64,256]{2,1,0:T(8,128)}, f32[128,128]{1,0:T(8,128)}) custom-call(f32[128,128]{1,0:T(8,128)S(1)} %get-tuple-element.4.g_ref, bf16[256,16384]{1,0:T(8,128)(2,1)S(1)} %get-tuple-element.5.m_ref), custom_call_target="tpu_custom_call" | custom-call | tf_op jit(solution)/shard_map/apply/pallas_call | solution.py:416

commit v4 on v3

--- a/solution.py
+++ b/solution.py
@@ -36,12 +36,9 @@
     load_k = pltpu.make_async_copy(k_hbm, kappa.at[own], load.at[rows])
     load_p = pltpu.make_async_copy(p_hbm, p_ref, load.at[rows + 1])
 
-    def begin(i, _):
+    load_k.start()
+    for i in range(rows):
         fetch(i).start()
-        return 0
-
-    load_k.start()
-    lax.fori_loop(0, rows, begin, 0)
     load_p.start()
     barrier = pltpu.get_barrier_semaphore()
     for d in range(1, nx):
@@ -58,17 +55,17 @@
     load_k.wait()
 
     def collect(q, pack):
-        for s in range(8):
-            fetch(q * 8 + s).wait()
-        for s in range(8):
-            i = q * 8 + s
+        for s in range(16):
+            fetch(q * 16 + s).wait()
+        for s in range(16):
+            i = q * 16 + s
             k_row = jnp.broadcast_to(kappa[pl.ds(i + 8, 1), :], (8, cols))
             first = jnp.concatenate([wide[i + 1, :, :128], k_row[:, :128]], 0)
             last = jnp.concatenate([wide[i + 1, :, cols - 128:], k_row[:, cols - 128:]], 0)
             pack = jnp.where(holder == i, pltpu.roll(jnp.where(packed == 0, first, last), 2 * i, 1), pack)
         return pack
 
-    edge[...] = lax.fori_loop(0, rows // 8, collect, jnp.zeros((modes + 8, 128), F32))
+    edge[...] = lax.fori_loop(0, rows // 16, collect, jnp.zeros((modes + 8, 128), F32))
 
     pl.semaphore_wait(barrier, nx + ny - 2)
     has_up, has_down, has_left, has_right = px > 0, px < nx - 1, py > 0, py < ny - 1
@@ -363,7 +360,7 @@
     yield
 
 
-def apply_kernel(g_ref, m_ref, o_hbm, r_ref, w_ref, upper, lower, out, sent):
+def apply_kernel(g_ref, m_ref, o_hbm, r_hbm, r_ref, w_ref, upper, lower, out, sent, kept):
     rows, columns, cols = out.shape
     half = columns // 2
     group = 16
@@ -395,6 +392,8 @@
 
     over(0, first, (rows,))
     next(steps)
+    keep = pltpu.make_async_copy(r_ref, r_hbm, kept)
+    keep.start()
     high, low = split(w_ref[half:, :])
     lower[:half, :columns] = high
     lower[:half, columns:] = high
@@ -407,6 +406,7 @@
 
     over(1, second, (rows // 2, rows // 4, rows // 4))
 
+    keep.wait()
     pltpu.make_async_copy(out, out, sent).wait()
 
 
@@ -420,12 +420,14 @@
             jax.ShapeDtypeStruct((columns, columns), F32),
         ),
         in_specs=[vmem, vmem],
-        out_specs=(pl.BlockSpec(memory_space=pltpu.HBM), vmem),
+        out_specs=(pl.BlockSpec(memory_space=pltpu.HBM),) * 2,
         scratch_shapes=[
+            pltpu.VMEM((columns, columns), F32),
             pltpu.VMEM((columns, columns), F32),
             pltpu.VMEM((columns // 2, 3 * columns // 2), BF16),
             pltpu.VMEM((columns, 2 * columns), BF16),
             pltpu.VMEM((rows, columns, cols), F32),
+            pltpu.SemaphoreType.DMA,
             pltpu.SemaphoreType.DMA,
         ],
         compiler_params=pltpu.CompilerParams(vmem_limit_bytes=20 * 1024 * 1024),

time: 31.4 us -> 30.5 us (0.971)
  Pallas kernels: 30.6 us -> 29.7 us
    pallas_call x1, Pallas kernels: 6.92 us -> 6.39 us  [apply(): pl.pallas_call(apply_kernel, out_shape=(jax.ShapeDtypeStruct((columns, ro...]
    pallas_call x1, Pallas kernels: 23.7 us -> 23.3 us  [gram(): pl.pallas_call(functools.partial(gram_kernel, nx, ny), out_shape=(pltpu.V...]
where the time goes in v4:
time: 30.5 us; the launch traced here: 30.3 us
  Pallas kernels  29.7 us (97%)
  between operations  0.64 us (2%)
    pallas_call x1, Pallas kernels, gram(): pl.pallas_call(functools.partial(gram_kernel, nx, ny), out_shape=(pltpu.V...  23.3 us
    pallas_call x1, Pallas kernels, apply(): pl.pallas_call(apply_kernel, out_shape=(jax.ShapeDtypeStruct((columns, ro...  6.39 us

profile of v4, /device:TPU:0, one launch (start us, length us, event | category | flops | bytes accessed | tf_op | source)
XLA Modules:
  0.0 30.3 jit_solution(3604939573578536353)
XLA Ops:
  0.6 23.3 %gram.1 = (bf16[256,16384]{1,0:T(8,128)(2,1)S(1)}, f32[128,128]{1,0:T(8,128)S(1)}) custom-call(f32[32,64,256]{2,1,0:T(8,128)} %u_hbm.1, f32[64,256]{1,0:T(8,128)} %k_hbm.1, f32[64,256]{1,0:T(8,128)} %p_hbm.1), custom_call_target="tpu_custom_call" | custom-call | tf_op jit(solution)/shard_map/gram/pallas_call | solution.py:259
  23.9 6.4 %apply.1 = (f32[128,64,256]{2,1,0:T(8,128)}, f32[128,128]{1,0:T(8,128)}) custom-call(f32[128,128]{1,0:T(8,128)S(1)} %get-tuple-element.4.g_ref, bf16[256,16384]{1,0:T(8,128)(2,1)S(1)} %get-tuple-element.5.m_ref), custom_call_target="tpu_custom_call" | custom-call | tf_op jit(solution)/shard_map/apply/pallas_call | solution.py:416

commit v5 on v4

--- a/solution.py
+++ b/solution.py
@@ -26,7 +26,7 @@
     modes = u_hbm.shape[0]
     tiles = cols // 128
     columns = 4 * modes
-    share = columns // ny
+    share = 3 * columns // 4 // ny
     px, py = lax.axis_index("gx"), lax.axis_index("gy")
 
     def fetch(i):
@@ -95,7 +95,7 @@
 
     def put(block, i, value):
         high, low = split(value)
-        at = pl.ds(pl.multiple_of(i * cols, cols), cols)
+        at = slice(i * cols, (i + 1) * cols) if isinstance(i, int) else pl.ds(pl.multiple_of(i * cols, cols), cols)
         m_ref[block * modes:(block + 1) * modes, at] = high
         m_ref[columns + block * modes:columns + (block + 1) * modes, at] = low
 
@@ -151,24 +151,17 @@
     inner(rows - group, group - 2, lax.fori_loop(0, rows // group - 1, sweep, flux(1)))
     lax.fori_loop(0, rows // group, stream, 0)
 
-    for copy, sends, receives in copies:
-        @pl.when(sends)
-        def _():
-            copy.wait_send()
-
-        @pl.when(receives)
-        def _():
-            copy.wait_recv()
-
-    @pl.when(px == 0)
-    def _():
-        wide[0] = jnp.zeros((modes, cols), F32)
-        kappa[pl.ds(0, 8), :] = jnp.zeros((8, cols), F32)
-
-    @pl.when(px == nx - 1)
-    def _():
-        wide[rows + 1] = jnp.zeros((modes, cols), F32)
-        kappa[pl.ds(rows + 8, 8), :] = jnp.zeros((8, cols), F32)
+    def settle(some):
+        for copy, sends, receives in some:
+            @pl.when(sends)
+            def _():
+                copy.wait_send()
+
+            @pl.when(receives)
+            def _():
+                copy.wait_recv()
+
+    settle(copies[4:])
 
     @pl.when(py == 0)
     def _():
@@ -178,34 +171,58 @@
     def _():
         halo[1] = jnp.zeros((modes + 8, 128), F32)
 
-    for i in (0, rows):
-        xface[i:i + 1, :] = 0.5 * (kappa[i + 7:i + 8, :] + kappa[i + 8:i + 9, :])
-    for i in (0, rows - 1):
-        put(1, i, flux(i + 1) - flux(i))
     mine = edge[...]
     other = jnp.where((packed & 1) == 0, pltpu.roll(halo[0], 1, 1), pltpu.roll(halo[1], 127, 1))
-    across = 0.5 * (mine[modes:modes + 1] + other[modes:modes + 1]) * (mine[:modes] - other[:modes])
-
+    border = 0.5 * (mine[modes:modes + 1] + other[modes:modes + 1]) * (mine[:modes] - other[:modes])
+
+    quarter = rows // 4
     acc[...] = jnp.zeros_like(acc)
 
+    def edges():
+        settle(copies[:4])
+
+        @pl.when(px == 0)
+        def _():
+            wide[0] = jnp.zeros((modes, cols), F32)
+            kappa[pl.ds(0, 8), :] = jnp.zeros((8, cols), F32)
+
+        @pl.when(px == nx - 1)
+        def _():
+            wide[rows + 1] = jnp.zeros((modes, cols), F32)
+            kappa[pl.ds(rows + 8, 8), :] = jnp.zeros((8, cols), F32)
+
+        for i in (0, rows):
+            xface[i:i + 1, :] = 0.5 * (kappa[i + 7:i + 8, :] + kappa[i + 8:i + 9, :])
+        for i in (0, rows - 1):
+            put(1, i, flux(i + 1) - flux(i))
+
     def build(g, _):
-        for s in range(32):
-            i = g * 32 + s
-            turn = pltpu.roll(across, (128 - 2 * i) & 127, 1)
-            b = [back[i, :, tile(t)] for t in range(tiles)]
-            y = [flow[i, :, tile(t)] - jnp.where(lanes == 0, b[t - 1], b[t]) for t in range(tiles)]
-            y[0] = y[0] + jnp.where(lanes == 0, turn, 0.0)
-            y[-1] = y[-1] + jnp.where(lanes == 127, turn, 0.0)
-            put(2, i, jnp.concatenate(y, 1))
-        at = pl.ds(pl.multiple_of(g * 32 * cols, 32 * cols), 32 * cols)
-        acc[...] += lax.dot_general(
-            m_ref[:, at], m_ref[:columns, at], (((1,), (1,)), ((), ())), preferred_element_type=F32
-        )
+        pl.when(g == 1)(edges)
+        starts = [(2 * g + 1) * quarter, lax.rem(2 * g + 2, 4) * quarter]
+        for first in starts:
+            for s in range(quarter):
+                i = first + s
+                turn = pltpu.roll(border, (128 - 2 * i) & 127, 1)
+                b = [back[i, :, tile(t)] for t in range(tiles)]
+                y = [flow[i, :, tile(t)] - jnp.where(lanes == 0, b[t - 1], b[t]) for t in range(tiles)]
+                y[0] = y[0] + jnp.where(lanes == 0, turn, 0.0)
+                y[-1] = y[-1] + jnp.where(lanes == 127, turn, 0.0)
+                put(2, i, jnp.concatenate(y, 1))
+        for first in starts:
+            at = pl.ds(pl.multiple_of(first * cols, quarter * cols), quarter * cols)
+            acc[...] += lax.dot_general(
+                m_ref[:, at], m_ref[:columns, at], (((1,), (1,)), ((), ())), preferred_element_type=F32
+            )
         return 0
 
-    lax.fori_loop(0, rows // 32, build, 0)
+    lax.fori_loop(0, 2, build, 0)
+    half = columns // 2
     cross = acc[columns:]
-    total = (acc[:columns] + (cross + cross.T)) * (1.0 / (rows * cols * nx * ny))
+    scale = 1.0 / (rows * cols * nx * ny)
+    upper = (acc[:half] + (cross[:half] + cross[:, :half].T)) * scale
+    corner = cross[half:, half:]
+    corner = (acc[half:columns, half:] + (corner + corner.T)) * scale
+    total = jnp.concatenate([upper, jnp.concatenate([corner[half // 2:], corner[:half // 2]], 1)], 0)
     for j in range(ny):
         part[j] = total[j * share:(j + 1) * share]
 
@@ -247,13 +264,17 @@
         copy.start()
     for copy in copies:
         copy.wait()
-    for j in range(ny):
-        g_ref[j * share:(j + 1) * share, :] = full[j]
+    whole = jnp.concatenate([full[j] for j in range(ny)], 0)
+    upper = whole[:half]
+    corner = jnp.concatenate([whole[half:, half:], whole[half:, :half]], 0)
+    g_ref[:half, :] = upper
+    g_ref[half:, :] = jnp.concatenate([upper[:, half:].T, corner], 1)
 
 
 def gram(fields, conduct, potential, nx, ny):
     modes, rows, cols = fields.shape
     columns = 4 * modes
+    share = 3 * columns // 4 // ny
     vmem = pl.BlockSpec(memory_space=pltpu.VMEM)
     dma = pltpu.SemaphoreType.DMA
     return pl.pallas_call(
@@ -276,10 +297,10 @@
             pltpu.VMEM((rows, modes, cols), F32),
             pltpu.VMEM((rows, modes, cols), F32),
             pltpu.VMEM((2 * columns, columns), F32),
-            pltpu.VMEM((ny, columns // ny, columns), F32),
-            pltpu.VMEM((ny, columns // ny, columns), F32),
-            pltpu.VMEM((nx, columns // ny, columns), F32),
-            pltpu.VMEM((ny, columns // ny, columns), F32),
+            pltpu.VMEM((ny, share, columns), F32),
+            pltpu.VMEM((ny, share, columns), F32),
+            pltpu.VMEM((nx, share, columns), F32),
+            pltpu.VMEM((ny, share, columns), F32),
             dma((rows + 2,)),
             dma((6,)), dma((6,)), dma((ny,)), dma((ny,)), dma((nx,)), dma((nx,)), dma((ny,)), dma((ny,)),
         ],
@@ -339,6 +360,8 @@
             line = row(plain[h], s) * root
             upper[h] = jnp.where(sub == s, line, upper[h])
             plain = [value if q < h else value - low[q] * line for q, value in enumerate(plain)]
+            if at >= size // 2:
+                yield
         for h in range(parts):
             first = at + h * block
             r_ref[first:first + block, :] = jnp.where(lane >= first + sub, upper[h], 0.0)
@@ -390,8 +413,14 @@
         right = jnp.concatenate([near, m_ref[columns:columns + half, at], near], 0)
         return jnp.dot(upper[...], right, preferred_element_type=F32)
 
-    over(0, first, (rows,))
-    next(steps)
+    def advance(i):
+        if i >= rows // 2:
+            next(steps)
+            next(steps)
+
+    over(0, first, (rows // 2, rows // 2), advance)
+    for _ in steps:
+        pass
     keep = pltpu.make_async_copy(r_ref, r_hbm, kept)
     keep.start()
     high, low = split(w_ref[half:, :])

time: 30.5 us -> 29.3 us (0.961)
  Pallas kernels: 29.7 us -> 28.5 us
    pallas_call x1, Pallas kernels: 23.3 us -> 22.4 us  [gram(): pl.pallas_call(functools.partial(gram_kernel, nx, ny), out_shape=(pltpu.V...]
where the time goes in v5:
time: 29.3 us; the launch traced here: 29.1 us
  Pallas kernels  28.5 us (97%)
  between operations  0.64 us (2%)
    pallas_call x1, Pallas kernels, gram(): pl.pallas_call(functools.partial(gram_kernel, nx, ny), out_shape=(pltpu.V...  22.4 us
    pallas_call x1, Pallas kernels, apply(): pl.pallas_call(apply_kernel, out_shape=(jax.ShapeDtypeStruct((columns, ro...  6.13 us

profile of v5, /device:TPU:0, one launch (start us, length us, event | category | flops | bytes accessed | tf_op | source)
XLA Modules:
  0.0 29.1 jit_solution(5680687329564226934)
XLA Ops:
  0.6 22.4 %gram.1 = (bf16[256,16384]{1,0:T(8,128)(2,1)S(1)}, f32[128,128]{1,0:T(8,128)S(1)}) custom-call(f32[32,64,256]{2,1,0:T(8,128)} %u_hbm.1, f32[64,256]{1,0:T(8,128)} %k_hbm.1, f32[64,256]{1,0:T(8,128)} %p_hbm.1), custom_call_target="tpu_custom_call" | custom-call | tf_op jit(solution)/shard_map/gram/pallas_call | solution.py:280
  23.0 6.1 %apply.1 = (f32[128,64,256]{2,1,0:T(8,128)}, f32[128,128]{1,0:T(8,128)}) custom-call(f32[128,128]{1,0:T(8,128)S(1)} %get-tuple-element.4.g_ref, bf16[256,16384]{1,0:T(8,128)(2,1)S(1)} %get-tuple-element.5.m_ref), custom_call_target="tpu_custom_call" | custom-call | tf_op jit(solution)/shard_map/apply/pallas_call | solution.py:445

commit v6 on v5

--- a/solution.py
+++ b/solution.py
@@ -37,14 +37,16 @@
     load_p = pltpu.make_async_copy(p_hbm, p_ref, load.at[rows + 1])
 
     load_k.start()
-    for i in range(rows):
+    for i in range(rows // 2):
         fetch(i).start()
-    load_p.start()
     barrier = pltpu.get_barrier_semaphore()
     for d in range(1, nx):
         pl.semaphore_signal(barrier, inc=1, device_id={"gx": lax.rem(px + d, nx)}, device_id_type=MESH)
     for d in range(1, ny):
         pl.semaphore_signal(barrier, inc=1, device_id={"gy": lax.rem(py + d, ny)}, device_id_type=MESH)
+    for i in range(rows // 2, rows):
+        fetch(i).start()
+    load_p.start()
 
     def iota(height):
         return lax.broadcasted_iota(jnp.int32, (height, 128), 1)
@@ -134,7 +136,7 @@
                 back[i, :, tile(t)] = pltpu.roll(f, 1, 1)
         return 0
 
-    group = 16
+    group = 32
 
     def inner(first, count, before):
         for s in range(group):

time: 29.3 us -> 29.3 us (level)
  no operation moved by 1% of the time
where the time goes in v6:
time: 29.3 us; the launch traced here: 29.1 us
  Pallas kernels  28.5 us (97%)
  between operations  0.64 us (2%)
    pallas_call x1, Pallas kernels, gram(): pl.pallas_call(functools.partial(gram_kernel, nx, ny), out_shape=(pltpu.V...  22.4 us
    pallas_call x1, Pallas kernels, apply(): pl.pallas_call(apply_kernel, out_shape=(jax.ShapeDtypeStruct((columns, ro...  6.13 us

profile of v6, /device:TPU:0, one launch (start us, length us, event | category | flops | bytes accessed | tf_op | source)
XLA Modules:
  0.0 29.1 jit_solution(14207998954093972197)
XLA Ops:
  0.6 22.4 %gram.1 = (bf16[256,16384]{1,0:T(8,128)(2,1)S(1)}, f32[128,128]{1,0:T(8,128)S(1)}) custom-call(f32[32,64,256]{2,1,0:T(8,128)} %u_hbm.1, f32[64,256]{1,0:T(8,128)} %k_hbm.1, f32[64,256]{1,0:T(8,128)} %p_hbm.1), custom_call_target="tpu_custom_call" | custom-call | tf_op jit(solution)/shard_map/gram/pallas_call | solution.py:282
  23.0 6.1 %apply.1 = (f32[128,64,256]{2,1,0:T(8,128)}, f32[128,128]{1,0:T(8,128)}) custom-call(f32[128,128]{1,0:T(8,128)S(1)} %get-tuple-element.4.g_ref, bf16[256,16384]{1,0:T(8,128)(2,1)S(1)} %get-tuple-element.5.m_ref), custom_call_target="tpu_custom_call" | custom-call | tf_op jit(solution)/shard_map/apply/pallas_call | solution.py:447

commit v7 on v6

--- a/solution.py
+++ b/solution.py
@@ -435,7 +435,7 @@
         both = jnp.dot(lower[...], m_ref[:, at], preferred_element_type=F32)
         return both[:half] + both[half:]
 
-    over(1, second, (rows // 2, rows // 4, rows // 4))
+    over(1, second, (rows // 4, rows // 2, rows // 4))
 
     keep.wait()
     pltpu.make_async_copy(out, out, sent).wait()

time: 29.3 us -> 29.3 us (level)
  no operation moved by 1% of the time
where the time goes in v7:
time: 29.3 us; the launch traced here: 29.1 us
  Pallas kernels  28.5 us (97%)
  between operations  0.64 us (2%)
    pallas_call x1, Pallas kernels, gram(): pl.pallas_call(functools.partial(gram_kernel, nx, ny), out_shape=(pltpu.V...  22.4 us
    pallas_call x1, Pallas kernels, apply(): pl.pallas_call(apply_kernel, out_shape=(jax.ShapeDtypeStruct((columns, ro...  6.12 us

profile of v7, /device:TPU:0, one launch (start us, length us, event | category | flops | bytes accessed | tf_op | source)
XLA Modules:
  0.0 29.1 jit_solution(9309727250651702301)
XLA Ops:
  0.6 22.4 %gram.1 = (bf16[256,16384]{1,0:T(8,128)(2,1)S(1)}, f32[128,128]{1,0:T(8,128)S(1)}) custom-call(f32[32,64,256]{2,1,0:T(8,128)} %u_hbm.1, f32[64,256]{1,0:T(8,128)} %k_hbm.1, f32[64,256]{1,0:T(8,128)} %p_hbm.1), custom_call_target="tpu_custom_call" | custom-call | tf_op jit(solution)/shard_map/gram/pallas_call | solution.py:282
  23.0 6.1 %apply.1 = (f32[128,64,256]{2,1,0:T(8,128)}, f32[128,128]{1,0:T(8,128)}) custom-call(f32[128,128]{1,0:T(8,128)S(1)} %get-tuple-element.4.g_ref, bf16[256,16384]{1,0:T(8,128)(2,1)S(1)} %get-tuple-element.5.m_ref), custom_call_target="tpu_custom_call" | custom-call | tf_op jit(solution)/shard_map/apply/pallas_call | solution.py:447
